TPU v7x, 8 devices: a whole 2x2x1 slice. The times are simulated.
8 devices in a mesh: hp: 2 (over z, y), cp: 4 (over x, core).
Axes of the slice: x: 2, y: 2, z: 1, core: 2. Of those that a mesh axis runs over, the one named last changes fastest.
Arguments:
- q: bfloat16 [8, 2048, 32, 128], P(None, ('cp', 'hp'))
- k: bfloat16 [8, 2048, 8, 128], P(None, ('cp', 'hp'))
- v: bfloat16 [8, 2048, 8, 128], P(None, ('cp', 'hp'))
- o: bfloat16 [8, 2048, 32, 128], P(None, ('cp', 'hp'))
- do: bfloat16 [8, 2048, 32, 128], P(None, ('cp', 'hp'))
- lse: float32 [8, 32, 2048], P(None, None, ('cp', 'hp'))
Outputs:
- output 1: bfloat16 [8, 2048, 32, 128], P(None, ('cp', 'hp'))
- output 2: bfloat16 [8, 2048, 8, 128], P(None, ('cp', 'hp'))
- output 3: bfloat16 [8, 2048, 8, 128], P(None, ('cp', 'hp'))
All inputs are finite; a program needn't handle non-finite values.
Results may differ from a plain program's by a relative error of at most 0.001.
Values are sent between devices in bfloat16 or wider.
A program may use at most 1 GiB of HBM per device.

v0:
```python
import jax
import jax.numpy as jnp
from jax import lax
from jax.sharding import PartitionSpec as P


def _block(q, do, lse, dlt, k, v, mask, scale):
    s = jnp.einsum('bqhgd,bkhd->bhgqk', q, k, preferred_element_type=jnp.float32) * scale
    p = jnp.exp(s - lse[..., None])
    if mask is not None:
        p = jnp.where(mask, p, 0.0)
    dv = jnp.einsum('bhgqk,bqhgd->bkhd', p.astype(jnp.bfloat16), do, preferred_element_type=jnp.float32)
    dp = jnp.einsum('bqhgd,bkhd->bhgqk', do, v, preferred_element_type=jnp.float32)
    ds = (p * (dp - dlt[..., None])).astype(jnp.bfloat16)
    dq = jnp.einsum('bhgqk,bkhd->bqhgd', ds, k, preferred_element_type=jnp.float32) * scale
    dk = jnp.einsum('bhgqk,bqhgd->bkhd', ds, q, preferred_element_type=jnp.float32) * scale
    return dq, dk, dv


def _own_step(q, do, lse, dlt, k, v, scale):
    c = q.shape[1] // 2
    tri = jnp.tril(jnp.ones((c, c), jnp.bool_))
    dq0, dk0, dv0 = _block(q[:, :c], do[:, :c], lse[..., :c], dlt[..., :c], k[:, :c], v[:, :c], tri, scale)
    m1 = jnp.concatenate([jnp.ones((c, c), jnp.bool_), tri], axis=1)
    dq1, dk1, dv1 = _block(q[:, c:], do[:, c:], lse[..., c:], dlt[..., c:], k, v, m1, scale)
    z = jnp.zeros_like(dk0)
    return (jnp.concatenate([dq0, dq1], axis=1), dk1 + jnp.concatenate([dk0, z], axis=1), dv1 + jnp.concatenate([dv0, z], axis=1))


def _remote_step(earlier, q, do, lse, dlt, k, v, scale):
    c = q.shape[1] // 2

    def first(ops):
        q, do, lse, dlt, k, v = ops
        dq, dk0, dv0 = _block(q, do, lse, dlt, k[:, :c], v[:, :c], None, scale)
        z = jnp.zeros_like(dk0)
        return dq, jnp.concatenate([dk0, z], axis=1), jnp.concatenate([dv0, z], axis=1)

    def second(ops):
        q, do, lse, dlt, k, v = ops
        dq1, dk, dv = _block(q[:, c:], do[:, c:], lse[..., c:], dlt[..., c:], k, v, None, scale)
        return jnp.concatenate([jnp.zeros_like(dq1), dq1], axis=1), dk, dv

    return lax.cond(earlier, first, second, (q, do, lse, dlt, k, v))


def solution(mesh):
    cp = mesh.shape['cp']
    seq = P(None, ('cp', 'hp'), None, None)
    stat = P(None, None, ('cp', 'hp'))
    perm = [(r, (r + 1) % cp) for r in range(cp)]

    def body(q, k, v, o, do, lse):
        i = lax.axis_index('cp')
        b, _, hq, d = q.shape
        scale = d ** -0.5
        dlt = jnp.sum(do.astype(jnp.float32) * o.astype(jnp.float32), axis=-1).transpose(0, 2, 1)
        st = lax.all_to_all(jnp.stack([lse, dlt]), 'hp', 2, 3, tiled=True)
        q, k, v, do = [lax.all_to_all(x, 'hp', 2, 1, tiled=True) for x in (q, k, v, do)]
        t, hk = k.shape[1], k.shape[2]
        g = q.shape[2] // hk
        q = q.reshape(b, t, hk, g, d)
        do = do.reshape(b, t, hk, g, d)
        lse_l = st[0].reshape(b, hk, g, t)
        dlt_l = st[1].reshape(b, hk, g, t)
        dq, dk, dv = _own_step(q, do, lse_l, dlt_l, k, v, scale)
        for s in range(1, cp):
            k, v, dk, dv = [lax.ppermute(x, 'cp', perm) for x in (k, v, dk, dv)]
            ddq, ddk, ddv = _remote_step(s <= i, q, do, lse_l, dlt_l, k, v, scale)
            dq, dk, dv = dq + ddq, dk + ddk, dv + ddv
        dk, dv = [lax.ppermute(x, 'cp', perm) for x in (dk, dv)]
        dq = dq.reshape(b, t, hk * g, d)
        return tuple(lax.all_to_all(x.astype(jnp.bfloat16), 'hp', 1, 2, tiled=True) for x in (dq, dk, dv))

    return jax.shard_map(body, mesh=mesh, in_specs=(seq, seq, seq, seq, seq, stat), out_specs=(seq, seq, seq), check_vma=False)
```

profile of v0, /device:TPU:0, one launch (start us, length us, event | category | flops | bytes accessed | tf_op | source)
XLA Modules:
  0.0 1968.3 jit_solution(10959902392870810239)
XLA Ops:
  42.9 41.5 %all-to-all-done = bf16[8,256,8,128]{3,1,0,2:T(8,128)(2,1)} async-done(((bf16[8,256,8,128]{3,1,0,2:T(8,128)(2,1)}), bf16[8,256,8,128]{3,1,0,2:T(8,128)(2,1)}, u32[]{:S(2)}, u32[]{:S(2)}) %all-to-all-start) | async-done | bytes 4194336 | tf_op jit(solution)/shard_map/all_to_all | solution.py:59
  105.2 30.9 %all-to-all-done.3 = bf16[8,256,8,128]{3,1,0,2:T(8,128)(2,1)} async-done(((bf16[8,256,8,128]{3,1,0,2:T(8,128)(2,1)}), bf16[8,256,8,128]{3,1,0,2:T(8,128)(2,1)}, u32[]{:S(2)}, u32[]{:S(2)}) %all-to-all-start.3) | async-done | bytes 4194336 | tf_op jit(solution)/shard_map/all_to_all | solution.py:59
  161.0 165.0 %all-to-all-done.1 = bf16[8,256,32,128]{3,1,0,2:T(8,128)(2,1)} async-done(((bf16[8,256,32,128]{3,1,0,2:T(8,128)(2,1)}), bf16[8,256,32,128]{3,1,0,2:T(8,128)(2,1)}, u32[]{:S(2)}, u32[]{:S(2)}) %all-to-all-start.1) | async-done | bytes 16777248 | tf_op jit(solution)/shard_map/all_to_all | solution.py:59
  361.0 154.5 %all-to-all-done.4 = bf16[8,256,32,128]{3,1,0,2:T(8,128)(2,1)} async-done(((bf16[8,256,32,128]{3,1,0,2:T(8,128)(2,1)}), bf16[8,256,32,128]{3,1,0,2:T(8,128)(2,1)}, u32[]{:S(2)}, u32[]{:S(2)}) %all-to-all-start.4) | async-done | bytes 16777248 | tf_op jit(solution)/shard_map/all_to_all | solution.py:59
  563.8 21.9 %fusion.147 = bf16[8,4,4,256,256]{3,4,2,1,0:T(8,128)(2,1)} fusion(f32[8,4,256,256,4]{3,2,4,1,0:T(8,128)} %fusion.170, f32[8,4,4,256]{3,2,1,0:T(4,128)S(1)} %get-tuple-element.136, f32[8,4,4,256]{3,2,1,0:T(4,128)S(1)} %get-tuple-element.131, pred[256,256]{0,1:T(8,128)(4,1)S(1)} %iota_compare_fusion, bf16[8,512,4,4,128]{4,1,3,2,0:T(8,128)(2,1)} %bitcast.444, ...), kind=kOutput, calls=%fused_computation.145 | convolution fusion | flops 2197815296 | bytes 61145088 | tf_op jit(solution)/shard_map/bqhgd,bkhd->bhgqk/dot_general | solution.py:13
  600.4 27.5 %fusion.164 = f32[8,4,512,256,4]{3,2,4,1,0:T(8,128)} fusion(bf16[8,512,4,128,1]{3,1,4,2,0:T(8,128)(2,1)} %bitcast.455, bf16[8,512,4,4,128]{4,1,3,2,0:T(8,128)(2,1)} %bitcast.435), kind=kOutput, calls=%fused_computation.167 | convolution fusion | flops 4294967296 | bytes 79691776 | tf_op jit(solution)/shard_map/bqhgd,bkhd->bhgqk/dot_general | solution.py:8
  628.0 40.0 %fusion.139 = bf16[8,4,4,256,512]{3,4,2,1,0:T(8,128)(2,1)} fusion(f32[8,4,512,256,4]{3,2,4,1,0:T(8,128)} %fusion.164, f32[8,4,4,256]{3,2,1,0:T(4,128)S(1)} %get-tuple-element.135, f32[8,4,4,256]{3,2,1,0:T(4,128)S(1)} %get-tuple-element.132, pred[256,512]{0,1:T(8,128)(4,1)S(1)} %concatenate.39, bf16[8,512,4,128,1]{3,1,4,2,0:T(8,128)(2,1)} %bitcast.461, ...), kind=kOutput, calls=%fused_computation.134 | convolution fusion | flops 4395630592 | bytes 113639424 | tf_op jit(solution)/shard_map/bqhgd,bkhd->bhgqk/dot_general | solution.py:13
  668.0 22.4 %bitcast_add_fusion.1 = f32[8,512,4,128]{3,1,2,0:T(8,128)} fusion(f32[8,256,4,128]{3,1,2,0:T(8,128)} %fusion.172, bf16[8,4,4,256,512]{3,4,2,1,0:T(8,128)(2,1)} %fusion.139, bf16[8,512,4,4,128]{4,1,3,2,0:T(8,128)(2,1)} %bitcast.436), kind=kOutput, calls=%fused_computation.161 | convolution fusion | flops 4299161600 | bytes 54525952 | tf_op jit(solution)/shard_map/bhgqk,bqhgd->bkhd/dot_general | solution.py:16
  690.4 30.7 %bitcast_add_fusion = f32[8,512,4,128]{3,1,2,0:T(8,128)} fusion(f32[8,256,4,128]{3,1,2,0:T(8,128)} %fusion.181, bf16[8,512,4,4,128]{4,1,3,2,0:T(8,128)(2,1)} %bitcast.446, f32[8,4,512,256,4]{3,2,4,1,0:T(8,128)} %fusion.164, f32[8,4,4,256]{3,2,1,0:T(4,128)S(1)} %get-tuple-element.132, pred[256,512]{0,1:T(8,128)(4,1)S(1)} %concatenate.39), kind=kOutput, calls=%fused_computation.160 | convolution fusion | flops 4364173312 | bytes 88342528 | tf_op jit(solution)/shard_map/bhgqk,bqhgd->bkhd/dot_general | solution.py:12
  723.2 194.8 %collective-permute-done.1 = bf16[8,512,4,128]{3,1,2,0:T(8,128)(2,1)} collective-permute-done((bf16[8,512,4,128]{3,1,2,0:T(8,128)(2,1)}, bf16[8,512,4,128]{3,1,2,0:T(8,128)(2,1)}, u32[]{:S(2)}, u32[]{:S(2)}) %collective-permute-start.1) | collective-permute-done | bytes 4194336 | tf_op jit(solution)/shard_map/ppermute | solution.py:68
  918.1 44.9 %collective-permute-done = bf16[8,512,4,128]{3,1,2,0:T(8,128)(2,1)} collective-permute-done((bf16[8,512,4,128]{3,1,2,0:T(8,128)(2,1)}, bf16[8,512,4,128]{3,1,2,0:T(8,128)(2,1)}, u32[]{:S(2)}, u32[]{:S(2)}) %collective-permute-start) | collective-permute-done | bytes 4194336 | tf_op jit(solution)/shard_map/ppermute | solution.py:68
  963.5 166.8 %conditional.3 = (f32[8,512,4,4,128]{4,1,3,2,0:T(8,128)}, f32[8,512,4,128]{3,1,2,0:T(8,128)}, f32[8,512,4,128]{3,1,2,0:T(8,128)}) conditional(s32[]{:T(128)} %convert_element_type.79, (bf16[8,512,4,4,128]{4,1,3,2,0:T(8,128)(2,1)}, bf16[8,512,4,128]{3,1,2,0:T(8,128)(2,1)}, f32[8,4,4,512]{3,2,1,0:T(4,128)S(1)}, bf16[8,512,4,4,128]{4,1,3,2,0:T(8,128)(2,1)}, ...), branch_computations={%region_1.2_spmd, %region_2.3_spmd} | conditional | flops 21618491392 | bytes 444334112 | solution.py:44
  963.5 28.0 %fusion.13 = f32[8,4,512,256,4]{3,2,4,1,0:T(8,128)} fusion(bf16[8,512,4,4,128]{4,1,3,2,0:T(8,128)(2,1)} %get-tuple-element.73, bf16[8,512,4,128]{3,1,2,0:T(8,128)(2,1)} %get-tuple-element.72), kind=kOutput, calls=%fused_computation.16 | convolution fusion | flops 4294967296 | bytes 79691776 | tf_op jit(solution)/shard_map/cond/branch_0_fun/bqhgd,bkhd->bhgqk/dot_general | solution.py:8
  991.6 29.4 %fusion.20 = f32[8,512,4,128]{3,1,2,0:T(8,128)} fusion(bf16[8,512,4,4,128]{4,1,3,2,0:T(8,128)(2,1)} %get-tuple-element.76, f32[8,4,512,256,4]{3,2,4,1,0:T(8,128)} %fusion.13, f32[8,4,4,256]{3,2,1,0:T(4,128)S(1)} %slice.65), kind=kOutput, calls=%fused_computation.21 | convolution fusion | flops 4345298944 | bytes 84017152 | tf_op jit(solution)/shard_map/cond/branch_0_fun/bhgqk,bqhgd->bkhd/dot_general | solution.py:12
  1021.0 38.6 %fusion.1 = bf16[8,4,4,256,512]{3,4,2,1,0:T(8,128)(2,1)} fusion(f32[8,4,512,256,4]{3,2,4,1,0:T(8,128)} %fusion.13, f32[8,4,4,256]{3,2,1,0:T(4,128)S(1)} %slice.67, f32[8,4,4,256]{3,2,1,0:T(4,128)S(1)} %slice.65, bf16[8,512,4,4,128]{4,1,3,2,0:T(8,128)(2,1)} %get-tuple-element.76, bf16[8,512,4,128]{3,1,2,0:T(8,128)(2,1)} %get-tuple-element.75), kind=kOutput, calls=%fused_computation.2 | convolution fusion | flops 4378853376 | bytes 113508352 | tf_op jit(solution)/shard_map/cond/branch_0_fun/bqhgd,bkhd->bhgqk/dot_general | solution.py:13
  1079.3 20.3 %multiply_bitcast_fusion = f32[8,256,4,4,128]{4,1,3,2,0:T(8,128)} fusion(bf16[8,4,4,256,512]{3,4,2,1,0:T(8,128)(2,1)} %fusion.1, bf16[8,512,4,128]{3,1,2,0:T(8,128)(2,1)} %get-tuple-element.72), kind=kOutput, calls=%fused_computation.9 | convolution fusion | flops 4299161600 | bytes 54525952 | tf_op jit(solution)/shard_map/cond/branch_0_fun/bhgqk,bkhd->bqhgd/dot_general | solution.py:15
  1165.5 20.3 %multiply_bitcast_fusion.6 = f32[8,256,4,4,128]{4,1,3,2,0:T(8,128)} fusion(bf16[8,4,4,256,512]{3,4,2,1,0:T(8,128)(2,1)} %fusion.139, bf16[8,512,4,128,1]{3,1,4,2,0:T(8,128)(2,1)} %bitcast.458), kind=kOutput, calls=%fused_computation.154 | convolution fusion | flops 4299161600 | bytes 54525952 | tf_op jit(solution)/shard_map/bhgqk,bkhd->bqhgd/dot_general | solution.py:15
  1185.8 166.9 %conditional.4 = (f32[8,512,4,4,128]{4,1,3,2,0:T(8,128)}, f32[8,512,4,128]{3,1,2,0:T(8,128)}, f32[8,512,4,128]{3,1,2,0:T(8,128)}) conditional(s32[]{:T(128)} %convert_element_type.80, (bf16[8,512,4,4,128]{4,1,3,2,0:T(8,128)(2,1)}, bf16[8,512,4,128]{3,1,2,0:T(8,128)(2,1)}, f32[8,4,4,512]{3,2,1,0:T(4,128)S(1)}, bf16[8,512,4,4,128]{4,1,3,2,0:T(8,128)(2,1)}, ...), branch_computations={%region_3.4_spmd, %region_4.5_spmd} | conditional | flops 21618491392 | bytes 444334112 | solution.py:44
  1186.0 27.6 %fusion.59 = f32[8,4,512,256,4]{3,2,4,1,0:T(8,128)} fusion(bf16[8,512,4,4,128]{4,1,3,2,0:T(8,128)(2,1)} %get-tuple-element.85, bf16[8,512,4,128]{3,1,2,0:T(8,128)(2,1)} %get-tuple-element.84), kind=kOutput, calls=%fused_computation.60 | convolution fusion | flops 4294967296 | bytes 79691776 | tf_op jit(solution)/shard_map/cond/branch_0_fun/bqhgd,bkhd->bhgqk/dot_general | solution.py:8
  1213.5 29.4 %fusion.66 = f32[8,512,4,128]{3,1,2,0:T(8,128)} fusion(bf16[8,512,4,4,128]{4,1,3,2,0:T(8,128)(2,1)} %get-tuple-element.88, f32[8,4,512,256,4]{3,2,4,1,0:T(8,128)} %fusion.59, f32[8,4,4,256]{3,2,1,0:T(4,128)S(1)} %slice.71), kind=kOutput, calls=%fused_computation.65 | convolution fusion | flops 4345298944 | bytes 84017152 | tf_op jit(solution)/shard_map/cond/branch_0_fun/bhgqk,bqhgd->bkhd/dot_general | solution.py:12
  1243.0 38.7 %fusion.47 = bf16[8,4,4,256,512]{3,4,2,1,0:T(8,128)(2,1)} fusion(f32[8,4,512,256,4]{3,2,4,1,0:T(8,128)} %fusion.59, f32[8,4,4,256]{3,2,1,0:T(4,128)S(1)} %slice.73, f32[8,4,4,256]{3,2,1,0:T(4,128)S(1)} %slice.71, bf16[8,512,4,4,128]{4,1,3,2,0:T(8,128)(2,1)} %get-tuple-element.88, bf16[8,512,4,128]{3,1,2,0:T(8,128)(2,1)} %get-tuple-element.87), kind=kOutput, calls=%fused_computation.46 | convolution fusion | flops 4378853376 | bytes 113508352 | tf_op jit(solution)/shard_map/cond/branch_0_fun/bqhgd,bkhd->bhgqk/dot_general | solution.py:13
  1368.3 44.9 %collective-permute-done.4 = bf16[8,512,4,128]{3,1,2,0:T(8,128)(2,1)} collective-permute-done((bf16[8,512,4,128]{3,1,2,0:T(8,128)(2,1)}, bf16[8,512,4,128]{3,1,2,0:T(8,128)(2,1)}, u32[]{:S(2)}, u32[]{:S(2)}) %collective-permute-start.4) | collective-permute-done | bytes 4194336 | tf_op jit(solution)/shard_map/ppermute | solution.py:68
  1413.2 169.2 %conditional.5 = (f32[8,512,4,4,128]{4,1,3,2,0:T(8,128)}, f32[8,512,4,128]{3,1,2,0:T(8,128)}, f32[8,512,4,128]{3,1,2,0:T(8,128)}) conditional(s32[]{:T(128)} %convert_element_type.81, (bf16[8,512,4,4,128]{4,1,3,2,0:T(8,128)(2,1)}, bf16[8,512,4,128]{3,1,2,0:T(8,128)(2,1)}, f32[8,4,4,512]{3,2,1,0:T(4,128)S(1)}, bf16[8,512,4,4,128]{4,1,3,2,0:T(8,128)(2,1)}, ...), branch_computations={%region_5.6_spmd, %region_6.7_spmd} | conditional | flops 21618491392 | bytes 444334112 | solution.py:44
  1413.3 27.6 %fusion.105 = f32[8,4,512,256,4]{3,2,4,1,0:T(8,128)} fusion(bf16[8,512,4,4,128]{4,1,3,2,0:T(8,128)(2,1)} %get-tuple-element.97, bf16[8,512,4,128]{3,1,2,0:T(8,128)(2,1)} %get-tuple-element.96), kind=kOutput, calls=%fused_computation.104 | convolution fusion | flops 4294967296 | bytes 79691776 | tf_op jit(solution)/shard_map/cond/branch_0_fun/bqhgd,bkhd->bhgqk/dot_general | solution.py:8
  1440.8 29.5 %fusion.112 = f32[8,512,4,128]{3,1,2,0:T(8,128)} fusion(bf16[8,512,4,4,128]{4,1,3,2,0:T(8,128)(2,1)} %get-tuple-element.100, f32[8,4,512,256,4]{3,2,4,1,0:T(8,128)} %fusion.105, f32[8,4,4,256]{3,2,1,0:T(4,128)S(1)} %slice.77), kind=kOutput, calls=%fused_computation.109 | convolution fusion | flops 4345298944 | bytes 84017152 | tf_op jit(solution)/shard_map/cond/branch_0_fun/bhgqk,bqhgd->bkhd/dot_general | solution.py:12
  1470.3 38.6 %fusion.93 = bf16[8,4,4,256,512]{3,4,2,1,0:T(8,128)(2,1)} fusion(f32[8,4,512,256,4]{3,2,4,1,0:T(8,128)} %fusion.105, f32[8,4,4,256]{3,2,1,0:T(4,128)S(1)} %slice.79, f32[8,4,4,256]{3,2,1,0:T(4,128)S(1)} %slice.77, bf16[8,512,4,4,128]{4,1,3,2,0:T(8,128)(2,1)} %get-tuple-element.100, bf16[8,512,4,128]{3,1,2,0:T(8,128)(2,1)} %get-tuple-element.99), kind=kOutput, calls=%fused_computation.90 | convolution fusion | flops 4378853376 | bytes 113508352 | tf_op jit(solution)/shard_map/cond/branch_0_fun/bqhgd,bkhd->bhgqk/dot_general | solution.py:13
  1603.2 47.3 %fusion.145 = bf16[8,512,4,4,128]{4,1,3,2,0:T(8,128)(2,1)} fusion(f32[8,512,4,4,128]{4,1,3,2,0:T(8,128)} %get-tuple-element.122, f32[8,512,4,4,128]{4,1,3,2,0:T(8,128)} %get-tuple-element.121, f32[8,512,4,4,128]{4,1,3,2,0:T(8,128)} %get-tuple-element.120, f32[8,256,4,4,128]{4,1,3,2,0:T(8,128)} %multiply_bitcast_fusion.6, ...), kind=kLoop, calls=%fused_computation.142 | loop fusion | flops 41943040 | bytes 150994944 | tf_op jit(solution)/shard_map/convert_element_type | solution.py:73
  1692.8 82.8 %collective-permute-done.12 = f32[8,512,4,128]{3,1,2,0:T(8,128)} collective-permute-done((f32[8,512,4,128]{3,1,2,0:T(8,128)}, f32[8,512,4,128]{3,1,2,0:T(8,128)}, u32[]{:S(2)}, u32[]{:S(2)}) %collective-permute-start.12) | collective-permute-done | bytes 8388640 | tf_op jit(solution)/shard_map/ppermute | solution.py:68
  1784.6 35.9 %collective-permute-done.9 = bf16[8,512,4,128]{3,1,2,0:T(8,128)(2,1)} collective-permute-done((bf16[8,512,4,128]{3,1,2,0:T(8,128)(2,1)S(1)}, bf16[8,512,4,128]{3,1,2,0:T(8,128)(2,1)}, u32[]{:S(2)}, u32[]{:S(2)}) %collective-permute-start.9) | collective-permute-done | bytes 4194336 | tf_op jit(solution)/shard_map/ppermute | solution.py:71
  1827.9 32.2 %all-to-all-done.5 = bf16[8,512,16,128]{3,2,0,1:T(8,128)(2,1)} async-done(((bf16[8,512,16,128]{3,2,0,1:T(8,128)(2,1)}), bf16[8,512,16,128]{3,2,0,1:T(8,128)(2,1)}, u32[]{:S(2)}, u32[]{:S(2)}) %all-to-all-start.5) | async-done | bytes 16777248 | tf_op jit(solution)/shard_map/all_to_all | solution.py:73
  1873.5 38.4 %all-to-all-done.6 = bf16[8,512,4,128]{3,2,0,1:T(4,128)(2,1)} async-done(((bf16[8,512,4,128]{3,2,0,1:T(4,128)(2,1)}), bf16[8,512,4,128]{3,2,0,1:T(4,128)(2,1)}, u32[]{:S(2)}, u32[]{:S(2)}) %all-to-all-start.6) | async-done | bytes 4194336 | tf_op jit(solution)/shard_map/all_to_all | solution.py:73
  1937.8 24.7 %all-to-all-done.7 = bf16[8,512,4,128]{3,2,0,1:T(4,128)(2,1)} async-done(((bf16[8,512,4,128]{3,2,0,1:T(4,128)(2,1)}), bf16[8,512,4,128]{3,2,0,1:T(4,128)(2,1)}, u32[]{:S(2)}, u32[]{:S(2)}) %all-to-all-start.7) | async-done | bytes 4194336 | tf_op jit(solution)/shard_map/all_to_all | solution.py:73
  (100 shorter events, 518.8 us)
Async XLA Ops:
  18.9 13.2 all-to-all-start.2
  32.1 52.4 %all-to-all-start = ((bf16[8,256,8,128]{3,1,0,2:T(8,128)(2,1)}), bf16[8,256,8,128]{3,1,0,2:T(8,128)(2,1)}, u32[]{:S(2)}, u32[]{:S(2)}) async-start(bf16[8,256,8,128]{3,1,0,2:T(8,128)(2,1)} %copy.87), calls=%async_computation | async-start | bytes 8388608 | tf_op jit(solution)/shard_map/all_to_all | solution.py:59
  84.5 51.6 %all-to-all-start.3 = ((bf16[8,256,8,128]{3,1,0,2:T(8,128)(2,1)}), bf16[8,256,8,128]{3,1,0,2:T(8,128)(2,1)}, u32[]{:S(2)}, u32[]{:S(2)}) async-start(bf16[8,256,8,128]{3,1,0,2:T(8,128)(2,1)} %copy.94), calls=%async_computation.3 | async-start | bytes 8388608 | tf_op jit(solution)/shard_map/all_to_all | solution.py:59
  136.1 189.8 %all-to-all-start.1 = ((bf16[8,256,32,128]{3,1,0,2:T(8,128)(2,1)}), bf16[8,256,32,128]{3,1,0,2:T(8,128)(2,1)}, u32[]{:S(2)}, u32[]{:S(2)}) async-start(bf16[8,256,32,128]{3,1,0,2:T(8,128)(2,1)} %copy.89), calls=%async_computation.1 | async-start | bytes 33554432 | tf_op jit(solution)/shard_map/all_to_all | solution.py:59
  325.9 189.6 %all-to-all-start.4 = ((bf16[8,256,32,128]{3,1,0,2:T(8,128)(2,1)}), bf16[8,256,32,128]{3,1,0,2:T(8,128)(2,1)}, u32[]{:S(2)}, u32[]{:S(2)}) async-start(bf16[8,256,32,128]{3,1,0,2:T(8,128)(2,1)} %copy.96), calls=%async_computation.4 | async-start | bytes 33554432 | tf_op jit(solution)/shard_map/all_to_all | solution.py:59
  336.2 0.7 copy-start.4
  336.5 24.5 %copy-start = (f32[8,4,4,512]{3,2,1,0:T(4,128)}, f32[8,4,4,512]{3,2,1,0:T(4,128)S(1)}, u32[]{:S(2)}) copy-start(f32[8,4,4,512]{3,2,1,0:T(4,128)S(1)} %reshape_squeeze.7) | copy-start | bytes 786436
  337.1 23.9 %copy-start.6 = (f32[1,8,16,2,256]{4,3,2,1,0:T(2,128)}, f32[1,8,16,2,256]{4,3,2,1,0:T(2,128)S(1)}, u32[]{:S(2)}) copy-start(f32[1,8,16,2,256]{4,3,2,1,0:T(2,128)S(1)} %copy.93) | copy-start | bytes 786436
  337.4 23.6 %copy-start.2 = (f32[8,4,4,512]{3,2,1,0:T(4,128)}, f32[8,4,4,512]{3,2,1,0:T(4,128)S(1)}, u32[]{:S(2)}) copy-start(f32[8,4,4,512]{3,2,1,0:T(4,128)S(1)} %reshape_squeeze.6) | copy-start | bytes 786436
  690.3 272.7 %copy-start.5 = (f32[1,8,16,2,256]{4,3,2,1,0:T(2,128)S(1)}, f32[1,8,16,2,256]{4,3,2,1,0:T(2,128)}, u32[]{:S(2)}) copy-start(f32[1,8,16,2,256]{4,3,2,1,0:T(2,128)} %copy-done.4) | copy-start | bytes 786436
  690.3 272.9 %copy-start.7 = (f32[1,8,16,2,256]{4,3,2,1,0:T(2,128)S(1)}, f32[1,8,16,2,256]{4,3,2,1,0:T(2,128)}, u32[]{:S(2)}) copy-start(f32[1,8,16,2,256]{4,3,2,1,0:T(2,128)} %copy-done.6) | copy-start | bytes 786436
  690.3 273.1 %copy-start.1 = (f32[8,4,4,512]{3,2,1,0:T(4,128)S(1)}, f32[8,4,4,512]{3,2,1,0:T(4,128)}, u32[]{:S(2)}) copy-start(f32[8,4,4,512]{3,2,1,0:T(4,128)} %copy-done) | copy-start | bytes 786436
  690.4 273.1 %copy-start.3 = (f32[8,4,4,512]{3,2,1,0:T(4,128)S(1)}, f32[8,4,4,512]{3,2,1,0:T(4,128)}, u32[]{:S(2)}) copy-start(f32[8,4,4,512]{3,2,1,0:T(4,128)} %copy-done.2) | copy-start | bytes 786436
  690.4 439.9 %collective-permute-start.6 = (f32[8,512,4,128]{3,1,2,0:T(8,128)}, f32[8,512,4,128]{3,1,2,0:T(8,128)}, u32[]{:S(2)}, u32[]{:S(2)}) collective-permute-start(f32[8,512,4,128]{3,1,2,0:T(8,128)} %bitcast_add_fusion.1), channel_id=1, source_target_pairs={{0,1},{1,2},{2,3},{3,0},{4,5},{5,6},{6,7},{7,4}} | collective-permute-start | bytes 25165832 | tf_op jit(solution)/shard_map/ppermute | solution.py:68
  721.1 419.5 %collective-permute-start.10 = (f32[8,512,4,128]{3,1,2,0:T(8,128)}, f32[8,512,4,128]{3,1,2,0:T(8,128)}, u32[]{:S(2)}, u32[]{:S(2)}) collective-permute-start(f32[8,512,4,128]{3,1,2,0:T(8,128)} %bitcast_add_fusion), channel_id=1, source_target_pairs={{0,1},{1,2},{2,3},{3,0},{4,5},{5,6},{6,7},{7,4}} | collective-permute-start | bytes 25165832 | tf_op jit(solution)/shard_map/ppermute | solution.py:68
  721.7 196.4 %collective-permute-start.1 = (bf16[8,512,4,128]{3,1,2,0:T(8,128)(2,1)}, bf16[8,512,4,128]{3,1,2,0:T(8,128)(2,1)}, u32[]{:S(2)}, u32[]{:S(2)}) collective-permute-start(bf16[8,512,4,128]{3,1,2,0:T(8,128)(2,1)} %bitcast.462), channel_id=1, source_target_pairs={{0,1},{1,2},{2,3},{3,0},{4,5},{5,6},{6,7},{7,4}} | collective-permute-start | bytes 12582920 | tf_op jit(solution)/shard_map/ppermute | solution.py:68
  721.8 241.2 %collective-permute-start = (bf16[8,512,4,128]{3,1,2,0:T(8,128)(2,1)}, bf16[8,512,4,128]{3,1,2,0:T(8,128)(2,1)}, u32[]{:S(2)}, u32[]{:S(2)}) collective-permute-start(bf16[8,512,4,128]{3,1,2,0:T(8,128)(2,1)} %bitcast.456), channel_id=1, source_target_pairs={{0,1},{1,2},{2,3},{3,0},{4,5},{5,6},{6,7},{7,4}} | collective-permute-start | bytes 12582920 | tf_op jit(solution)/shard_map/ppermute | solution.py:68
  918.1 232.9 %collective-permute-start.3 = (bf16[8,512,4,128]{3,1,2,0:T(8,128)(2,1)}, bf16[8,512,4,128]{3,1,2,0:T(8,128)(2,1)}, u32[]{:S(2)}, u32[]{:S(2)}) collective-permute-start(bf16[8,512,4,128]{3,1,2,0:T(8,128)(2,1)} %collective-permute-done.1), channel_id=1, source_target_pairs={{0,1},{1,2},{2,3},{3,0},{4,5},{5,6},{6,7},{7,4}} | collective-permute-start | bytes 12582920 | tf_op jit(solution)/shard_map/ppermute | solution.py:68
  963.0 188.5 %collective-permute-start.2 = (bf16[8,512,4,128]{3,1,2,0:T(8,128)(2,1)}, bf16[8,512,4,128]{3,1,2,0:T(8,128)(2,1)}, u32[]{:S(2)}, u32[]{:S(2)}) collective-permute-start(bf16[8,512,4,128]{3,1,2,0:T(8,128)(2,1)} %collective-permute-done), channel_id=1, source_target_pairs={{0,1},{1,2},{2,3},{3,0},{4,5},{5,6},{6,7},{7,4}} | collective-permute-start | bytes 12582920 | tf_op jit(solution)/shard_map/ppermute | solution.py:68
  1140.6 441.9 %collective-permute-start.7 = (f32[8,512,4,128]{3,1,2,0:T(8,128)}, f32[8,512,4,128]{3,1,2,0:T(8,128)}, u32[]{:S(2)}, u32[]{:S(2)}) collective-permute-start(f32[8,512,4,128]{3,1,2,0:T(8,128)} %add.59), channel_id=1, source_target_pairs={{0,1},{1,2},{2,3},{3,0},{4,5},{5,6},{6,7},{7,4}} | collective-permute-start | bytes 25165832 | tf_op jit(solution)/shard_map/ppermute | solution.py:68
  1151.0 441.8 %collective-permute-start.11 = (f32[8,512,4,128]{3,1,2,0:T(8,128)}, f32[8,512,4,128]{3,1,2,0:T(8,128)}, u32[]{:S(2)}, u32[]{:S(2)}) collective-permute-start(f32[8,512,4,128]{3,1,2,0:T(8,128)} %add.63), channel_id=1, source_target_pairs={{0,1},{1,2},{2,3},{3,0},{4,5},{5,6},{6,7},{7,4}} | collective-permute-start | bytes 25165832 | tf_op jit(solution)/shard_map/ppermute | solution.py:68
  1151.0 217.3 %collective-permute-start.5 = (bf16[8,512,4,128]{3,1,2,0:T(8,128)(2,1)}, bf16[8,512,4,128]{3,1,2,0:T(8,128)(2,1)}, u32[]{:S(2)}, u32[]{:S(2)}) collective-permute-start(bf16[8,512,4,128]{3,1,2,0:T(8,128)(2,1)} %collective-permute-done.3), channel_id=1, source_target_pairs={{0,1},{1,2},{2,3},{3,0},{4,5},{5,6},{6,7},{7,4}} | collective-permute-start | bytes 12582920 | tf_op jit(solution)/shard_map/ppermute | solution.py:68
  1151.5 261.7 %collective-permute-start.4 = (bf16[8,512,4,128]{3,1,2,0:T(8,128)(2,1)}, bf16[8,512,4,128]{3,1,2,0:T(8,128)(2,1)}, u32[]{:S(2)}, u32[]{:S(2)}) collective-permute-start(bf16[8,512,4,128]{3,1,2,0:T(8,128)(2,1)} %collective-permute-done.2), channel_id=1, source_target_pairs={{0,1},{1,2},{2,3},{3,0},{4,5},{5,6},{6,7},{7,4}} | collective-permute-start | bytes 12582920 | tf_op jit(solution)/shard_map/ppermute | solution.py:68
  1592.8 92.9 %collective-permute-start.8 = (f32[8,512,4,128]{3,1,2,0:T(8,128)}, f32[8,512,4,128]{3,1,2,0:T(8,128)}, u32[]{:S(2)}, u32[]{:S(2)}) collective-permute-start(f32[8,512,4,128]{3,1,2,0:T(8,128)} %add.60), channel_id=1, source_target_pairs={{0,1},{1,2},{2,3},{3,0},{4,5},{5,6},{6,7},{7,4}} | collective-permute-start | bytes 25165832 | tf_op jit(solution)/shard_map/ppermute | solution.py:68
  1603.2 172.4 %collective-permute-start.12 = (f32[8,512,4,128]{3,1,2,0:T(8,128)}, f32[8,512,4,128]{3,1,2,0:T(8,128)}, u32[]{:S(2)}, u32[]{:S(2)}) collective-permute-start(f32[8,512,4,128]{3,1,2,0:T(8,128)} %add.64), channel_id=1, source_target_pairs={{0,1},{1,2},{2,3},{3,0},{4,5},{5,6},{6,7},{7,4}} | collective-permute-start | bytes 25165832 | tf_op jit(solution)/shard_map/ppermute | solution.py:68
  1669.1 191.1 %all-to-all-start.5 = ((bf16[8,512,16,128]{3,2,0,1:T(8,128)(2,1)}), bf16[8,512,16,128]{3,2,0,1:T(8,128)(2,1)}, u32[]{:S(2)}, u32[]{:S(2)}) async-start(bf16[8,512,16,128]{3,2,0,1:T(8,128)(2,1)} %copy.103), calls=%async_computation.5 | async-start | bytes 33554432 | tf_op jit(solution)/shard_map/all_to_all | solution.py:73
  1692.7 127.8 %collective-permute-start.9 = (bf16[8,512,4,128]{3,1,2,0:T(8,128)(2,1)S(1)}, bf16[8,512,4,128]{3,1,2,0:T(8,128)(2,1)}, u32[]{:S(2)}, u32[]{:S(2)}) collective-permute-start(bf16[8,512,4,128]{3,1,2,0:T(8,128)(2,1)S(1)} %add.61), channel_id=1, source_target_pairs={{0,1},{1,2},{2,3},{3,0},{4,5},{5,6},{6,7},{7,4}} | collective-permute-start | bytes 12582920 | tf_op jit(solution)/shard_map/ppermute | solution.py:71
  1784.6 81.4 %collective-permute-start.13 = (bf16[8,512,4,128]{3,1,2,0:T(8,128)(2,1)}, bf16[8,512,4,128]{3,1,2,0:T(8,128)(2,1)}, u32[]{:S(2)}, u32[]{:S(2)}) collective-permute-start(bf16[8,512,4,128]{3,1,2,0:T(8,128)(2,1)} %add.65), channel_id=1, source_target_pairs={{0,1},{1,2},{2,3},{3,0},{4,5},{5,6},{6,7},{7,4}} | collective-permute-start | bytes 12582920 | tf_op jit(solution)/shard_map/ppermute | solution.py:71
  1860.2 51.6 %all-to-all-start.6 = ((bf16[8,512,4,128]{3,2,0,1:T(4,128)(2,1)}), bf16[8,512,4,128]{3,2,0,1:T(4,128)(2,1)}, u32[]{:S(2)}, u32[]{:S(2)}) async-start(bf16[8,512,4,128]{3,2,0,1:T(4,128)(2,1)} %copy.105), calls=%async_computation.6 | async-start | bytes 8388608 | tf_op jit(solution)/shard_map/all_to_all | solution.py:73
  1911.8 50.7 %all-to-all-start.7 = ((bf16[8,512,4,128]{3,2,0,1:T(4,128)(2,1)}), bf16[8,512,4,128]{3,2,0,1:T(4,128)(2,1)}, u32[]{:S(2)}, u32[]{:S(2)}) async-start(bf16[8,512,4,128]{3,2,0,1:T(4,128)(2,1)} %copy.107), calls=%async_computation.7 | async-start | bytes 8388608 | tf_op jit(solution)/shard_map/all_to_all | solution.py:73
where the time goes:
time: 1980 us; the launch traced here: 1970 us
  waiting for transfers between devices  916 us (46%)
  matrix products  631 us (32%)
  local copies, waits for them, and re-layouts  198 us (10%)
  other arithmetic  120 us (6%)
  starting transfers between devices  61.1 us (3%)
  loops' own time  39.9 us (2%)
    all_to_all x4, waiting for transfers between devices, body(): lax.all_to_all(x, 'hp', 2, 1, tiled=True)  392 us
    ppermute x12, waiting for transfers between devices, body(): k, v, dk, dv = [lax.ppermute(x, 'cp', perm) for x in (k, v, dk, dv)]  390 us
    dot_general x5, matrix products, _block(): jnp.einsum('bqhgd,bkhd->bhgqk', do, v, preferred_element_type=jnp.float32)  178 us
    dot_general x5, matrix products, _block(): jnp.einsum('bhgqk,bqhgd->bkhd', p.astype(jnp.bfloat16), do, preferred_ele...  137 us
    dot_general x5, matrix products, _block(): jnp.einsum('bqhgd,bkhd->bhgqk', q, k, preferred_element_type=jnp.float32)  127 us
    dot_general x5, matrix products, _block(): jnp.einsum('bhgqk,bqhgd->bkhd', ds, q, preferred_element_type=jnp.float32)  96.2 us
    all_to_all x3, waiting for transfers between devices, body(): lax.all_to_all(x.astype(jnp.bfloat16), 'hp', 1, 2, tiled=True)  95.3 us
    dot_general x5, matrix products, _block(): jnp.einsum('bhgqk,bkhd->bqhgd', ds, k, preferred_element_type=jnp.float32)  93.4 us
  transfers between devices with their start and end apart: 22, of which 15 were waited for; matrix products, arithmetic and copies ran while one was open for 38% of the time, Pallas kernels for 0%

commit v1 on v0

v1 whole, which is shorter than its diff:
```python
import functools

import jax
import jax.numpy as jnp
from jax import lax
from jax.experimental import pallas as pl
from jax.experimental.layout import Layout, with_layout_constraint
from jax.experimental.pallas import tpu as pltpu
from jax.sharding import PartitionSpec as P

AXES = ('cp', 'hp')
CHUNKS = (1, 2, 2, 2, 1)
ORDER = (
    ('in', 0, ()), ('in', 1, ()), ('stat', 0, ()), ('in', 2, ()), ('out', 0, ()), ('in', 3, (0,)), ('out', 1, ()),
    ('out', 2, (1,)), ('in', 4, ()), ('out', 3, (2,)), ('out', 4, (3,)),
)


def _dot(a, b, ca, cb):
    return lax.dot_general(a, b, (((ca,), (cb,)), ((), ())), preferred_element_type=jnp.float32)


def _kernel(n, g, scale, q_ref, do_ref, kv_ref, st_ref, out_ref, dk_ref, dv_ref, dq_ref):
    i = pl.program_id(1)
    t, d = q_ref.shape[-2:]

    def stored(j):
        return jnp.where(j < n // 2, 2 * j, 2 * n - 1 - 2 * j)

    @pl.when(i == 0)
    def _():
        dk_ref[...] = jnp.zeros_like(dk_ref)
        dv_ref[...] = jnp.zeros_like(dv_ref)

    dq_ref[...] = jnp.zeros_like(dq_ref)

    def step(j, diagonal):
        c = stored(j)
        q = q_ref[0, 0].reshape(g * t, d)
        do = do_ref[0, 0].reshape(g * t, d)
        k = kv_ref[c, 0, 0]
        v = kv_ref[c, 0, 1]
        p = jnp.exp(_dot(k, q, 1, 1) * scale - st_ref[0, 0, 0:1, :])
        if diagonal:
            key = lax.broadcasted_iota(jnp.int32, p.shape, 0)
            query = lax.broadcasted_iota(jnp.int32, p.shape, 1) & (t - 1)
            p = jnp.where(key <= query, p, 0.0)
        dv_ref[j] += _dot(p.astype(jnp.bfloat16), do, 1, 0)
        dp = _dot(v, do, 1, 1)
        ds = (p * (dp - st_ref[0, 0, 1:2, :])).astype(jnp.bfloat16)
        dk_ref[j] += _dot(ds, q, 1, 0)
        dq_ref[...] += _dot(ds, k, 0, 0)

    lax.fori_loop(0, i, lambda j, _: step(j, False), None)
    step(i, True)
    out_ref[stored(i), 0, 0:g] = (dq_ref[...] * scale).reshape(g, t, d).astype(out_ref.dtype)

    @pl.when(i == n - 1)
    def _():
        for j in range(n):
            c = 2 * j if j < n // 2 else 2 * n - 1 - 2 * j
            out_ref[c, 0, g] = (dk_ref[j] * scale).astype(out_ref.dtype)
            out_ref[c, 0, g + 1] = dv_ref[j].astype(out_ref.dtype)


def _attend(x, st, first, g, scale):
    n, nb, _, t, d = x.shape

    def stored(i):
        return jnp.where(i < n // 2, 2 * i, 2 * n - 1 - 2 * i)

    pairs = nb * n * (n + 1) // 2 * g * t * t
    return pl.pallas_call(
        functools.partial(_kernel, n, g, scale),
        grid=(nb, n),
        in_specs=[
            pl.BlockSpec((1, 1, g, t, d), lambda b, i: (stored(i), b, 0, 0, 0)),
            pl.BlockSpec((1, 1, g, t, d), lambda b, i: (stored(i), b, 1, 0, 0)),
            pl.BlockSpec((n, 1, 2, t, d), lambda b, i: (0, b, g, 0, 0)),
            pl.BlockSpec((1, 1, 2, g * t), lambda b, i: (stored(i), b + first, 0, 0)),
        ],
        out_specs=pl.BlockSpec((n, 1, g + 2, t, d), lambda b, i: (0, b, 0, 0, 0)),
        out_shape=jax.ShapeDtypeStruct((n, nb, g + 2, t, d), jnp.bfloat16),
        scratch_shapes=[
            pltpu.VMEM((n, t, d), jnp.float32),
            pltpu.VMEM((n, t, d), jnp.float32),
            pltpu.VMEM((g * t, d), jnp.float32),
        ],
        compiler_params=pltpu.CompilerParams(dimension_semantics=('arbitrary', 'arbitrary')),
        cost_estimate=pl.CostEstimate(flops=10 * pairs * d, bytes_accessed=x.size * 4, transcendentals=pairs),
        name='attend',
    )(x, x, x, st)


def solution(mesh):
    n = mesh.shape['cp'] * mesh.shape['hp']
    seq = P(None, AXES, None, None)
    stat = P(None, None, AXES)

    def body(q, k, v, o, do, lse):
        b, t, hq, d = q.shape
        hk = k.shape[2]
        g = hq // hk
        scale = d ** -0.5

        def heads(x, lo, hi):
            x = x[lo:hi]
            return x.reshape(hi - lo, t, hk, -1, d).transpose(2, 0, 3, 1, 4)

        def exchange(x):
            return lax.all_to_all(x, AXES, 0, 0, tiled=True)

        bounds = []
        lo = 0
        for size in CHUNKS:
            bounds.append((lo, lo + size))
            lo += size

        def pack(c):
            return jnp.concatenate([heads(x, *bounds[c]) for x in (q, do, k, v)], axis=2)

        def rows(x):
            return with_layout_constraint(x, Layout(major_to_minor=(0, 1, 2, 3)))

        def unpack(y, c, outs):
            lo, hi = bounds[c]
            new = [
                rows(y[:, :, :g].transpose(1, 3, 0, 2, 4).reshape(hi - lo, t, hq, d)),
                rows(y[:, :, g].transpose(1, 2, 0, 3)),
                rows(y[:, :, g + 1].transpose(1, 2, 0, 3)),
            ]
            if outs is None:
                zero = jnp.zeros((), q.dtype)
                return [lax.pad(x, zero, [(lo, b - hi, 0)] + [(0, 0, 0)] * 3) for x in new]
            return [lax.dynamic_update_slice(out, x, (lo, 0, 0, 0)) for out, x in zip(outs, new)]

        got, back, ahead, st, outs, last, prev = {}, {}, {}, None, None, None, None
        for kind, c, done in ORDER:
            if kind == 'in':
                x = ahead[c] if c in ahead else pack(c)
            elif kind == 'out':
                x = _attend(got[c], st, bounds[c][0], g, scale)
            else:
                dlt = jnp.sum(do.astype(jnp.float32) * o.astype(jnp.float32), axis=-1).transpose(0, 2, 1)
                x = jnp.stack([z.reshape(b, hk, g * t).transpose(1, 0, 2) for z in (lse, dlt)], axis=2)
                x, ahead[2] = lax.optimization_barrier((x, pack(2)))
            if last is not None:
                x, last, outs = lax.optimization_barrier((x, last, outs))
                if prev[0] == 'in':
                    got[prev[1]] = last
                elif prev[0] == 'out':
                    back[prev[1]] = last
                else:
                    st = last
            for e in done:
                back[e], x = lax.optimization_barrier((back[e], x))
                outs = unpack(back[e], e, outs)
            last = exchange(x)
            if kind == 'out':
                last = with_layout_constraint(last, Layout(major_to_minor=(0, 1, 2, 3, 4)))
            prev = kind, c
        dq, dk, dv = unpack(last, prev[1], outs)
        return dq, dk, dv

    return jax.shard_map(body, mesh=mesh, in_specs=(seq, seq, seq, seq, seq, stat), out_specs=(seq, seq, seq), check_vma=False)
```

time: 1980 us -> 837 us (0.42)
  matrix products: 631 us -> 0 us
  waiting for transfers between devices: 916 us -> 317 us
  Pallas kernels: 0 us -> 286 us
  other arithmetic: 120 us -> 49.8 us
  local copies, waits for them, and re-layouts: 198 us -> 131 us
  loops' own time: 39.9 us -> 0 us
  starting transfers between devices: 61.1 us -> 36.6 us
    dot_general x25 -> x0, matrix products: 631 us -> none  [the longest x5 178 us: _block(): jnp.einsum('bqhgd,bkhd->bhgqk', do, v, preferred_element_type=jnp.float32)]
    ppermute x14 -> x0, waiting for transfers between devices: 426 us -> none  [the longest x12 390 us: body(): k, v, dk, dv = [lax.ppermute(x, 'cp', perm) for x in (k, v, dk, dv)]]
    pallas_call x0 -> x5, Pallas kernels: none -> 286 us  [_attend(): pl.pallas_call(functools.partial(_kernel, n, g, scale), grid=(nb, n), in_...]
    all_to_all x8 -> x10, waiting for transfers between devices: 490 us -> 317 us  [exchange(): return lax.all_to_all(x, AXES, 0, 0, tiled=True)]
    all_to_all x7 -> x0, local copies, waits for them, and re-layouts: 63.6 us -> none  [the longest x4 37.6 us: body(): lax.all_to_all(x, 'hp', 2, 1, tiled=True)]
    add x6 -> x0, other arithmetic: 57.5 us -> none  [body(): dq, dk, dv = (dq + ddq, dk + ddk, dv + ddv)]
    concatenate x4 -> x0, local copies, waits for them, and re-layouts: 55.6 us -> none  [the longest x3 55.5 us: second(): return (jnp.concatenate([jnp.zeros_like(dq1), dq1], axis=1), dk, dv)]
    convert_element_type x1 -> x0, other arithmetic: 47.3 us -> none  [body(): x.astype(jnp.bfloat16)]
  transfers between devices with their start and end apart: 22 -> 10, of which waited for: 15 -> 8; matrix products, arithmetic and copies ran while one was open for 38% -> 18% of each run, Pallas kernels for 0% -> 34%
where the time goes in v1:
time: 837 us; the launch traced here: 833 us
  waiting for transfers between devices  317 us (38%)
  Pallas kernels  286 us (34%)
  local copies, waits for them, and re-layouts  131 us (16%)
  other arithmetic  49.8 us (6%)
  starting transfers between devices  36.6 us (4%)
  blocking collectives  10.5 us (1%)
    all_to_all x10, waiting for transfers between devices, exchange(): return lax.all_to_all(x, AXES, 0, 0, tiled=True)  317 us
    pallas_call x5, Pallas kernels, _attend(): pl.pallas_call(functools.partial(_kernel, n, g, scale), grid=(nb, n), in_...  286 us
    all_to_all x10, starting transfers between devices, exchange(): return lax.all_to_all(x, AXES, 0, 0, tiled=True)  36.6 us
    concatenate x5, other arithmetic, pack(): jnp.concatenate([heads(x, *bounds[c]) for x in (q, do, k, v)], axis=2)  34 us
    slice x12, local copies, waits for them, and re-layouts, heads(): x = x[lo:hi]  31.2 us
    optimization_barrier x4, local copies, waits for them, and re-layouts, body(): back[e], x = lax.optimization_barrier((back[e], x))  25.1 us
    transpose x10, local copies, waits for them, and re-layouts, unpack(): y[:, :, :g].transpose(1, 3, 0, 2, 4).reshape(hi - lo, t, hq, d)  20.8 us
    unnamed x38, local copies, waits for them, and re-layouts  19.6 us
  transfers between devices with their start and end apart: 10, of which 8 were waited for; matrix products, arithmetic and copies ran while one was open for 18% of the time, Pallas kernels for 34%

profile of v1, /device:TPU:0, one launch (start us, length us, event | category | flops | bytes accessed | tf_op | source)
XLA Modules:
  0.0 832.9 jit_solution(6144575937745768973)
XLA Ops:
  4.8 4.3 fusion.8
  9.9 4.3 fusion.9
  18.2 4.5 all-to-all-start
  22.8 8.4 %fusion.10 = (bf16[2,256,32,128]{3,2,1,0:T(8,128)(2,1)}, bf16[2,256,32,128]{3,2,1,0:T(8,128)(2,1)S(1)}, bf16[2,256,32,128]{3,2,1,0:T(8,128)(2,1)}) fusion(bf16[8,256,32,128]{3,2,1,0:T(8,128)(2,1)} %param.6), kind=kLoop, calls=%fused_computation.54 | loop fusion | bytes 25165824 | tf_op jit(solution)/shard_map/slice | solution.py:107
  35.3 4.4 fusion.11
  47.2 9.2 %pad_maximum_fusion.1 = bf16[8,2,10,256,128]{4,3,2,1,0:T(8,128)(2,1)} fusion(bf16[8,2,1,256,128]{4,3,2,1,0:T(8,128)(2,1)S(1)} %get-tuple-element.129, bf16[8,2,1,256,128]{4,3,2,1,0:T(8,128)(2,1)S(1)} %get-tuple-element.130, bf16[8,2,4,256,128]{4,3,2,1,0:T(8,128)(2,1)S(1)} %get-tuple-element.127, bf16[8,2,4,256,128]{4,3,2,1,0:T(8,128)(2,1)S(1)} %get-tuple-element.128), kind=kLoop, calls=%fused_computation.2 | loop fusion | flops 15728640 | bytes 20971520 | tf_op jit(solution)/shard_map/concatenate | solution.py:120
  56.5 25.5 %all-to-all-done.q_ref.do_ref.kv_ref = bf16[8,1,10,256,128]{4,3,2,1,0:T(8,128)(2,1)} async-done(((bf16[8,1,10,256,128]{4,3,2,1,0:T(8,128)(2,1)}), bf16[8,1,10,256,128]{4,3,2,1,0:T(8,128)(2,1)}, u32[]{:S(2)}, u32[]{:S(2)}) %all-to-all-start) | async-done | bytes 5242912 | tf_op jit(solution)/shard_map/all_to_all | solution.py:111
  82.0 4.1 all-to-all-start.1
  87.3 15.4 %multiply_reduce_fusion = f32[8,256,32]{2,1,0:T(8,128)S(1)} fusion(bf16[8,256,32,128]{3,2,1,0:T(8,128)(2,1)} %param.9, bf16[8,256,32,128]{3,2,1,0:T(8,128)(2,1)} %param.10), kind=kLoop, calls=%fused_computation | loop fusion | flops 33488896 | bytes 33816576 | tf_op jit(solution)/shard_map/reduce_sum | solution.py:144
  103.4 4.0 copy.125
  111.1 9.3 %pad_maximum_fusion = bf16[8,2,10,256,128]{4,3,2,1,0:T(8,128)(2,1)} fusion(bf16[8,2,1,256,128]{4,3,2,1,0:T(8,128)(2,1)S(1)} %get-tuple-element.125, bf16[8,2,1,256,128]{4,3,2,1,0:T(8,128)(2,1)S(1)} %get-tuple-element.126, bf16[8,2,4,256,128]{4,3,2,1,0:T(8,128)(2,1)S(1)} %get-tuple-element.123, bf16[8,2,4,256,128]{4,3,2,1,0:T(8,128)(2,1)S(1)} %get-tuple-element.124), kind=kLoop, calls=%fused_computation.1 | loop fusion | flops 15728640 | bytes 20971520 | tf_op jit(solution)/shard_map/concatenate | solution.py:120
  120.4 81.1 %all-to-all-done.1.q_ref.do_ref.kv_ref = bf16[8,2,10,256,128]{4,3,2,1,0:T(8,128)(2,1)} async-done(((bf16[8,2,10,256,128]{4,3,2,1,0:T(8,128)(2,1)}), bf16[8,2,10,256,128]{4,3,2,1,0:T(8,128)(2,1)}, u32[]{:S(2)}, u32[]{:S(2)}) %all-to-all-start.1) | async-done | bytes 10485792 | tf_op jit(solution)/shard_map/all_to_all | solution.py:111
  201.5 10.5 %all_to_all.55.st_ref = f32[8,8,2,1024]{3,2,1,0:T(2,128)} all-to-all(f32[8,8,2,1024]{3,2,1,0:T(2,128)S(1)} %pad_maximum_fusion.5), channel_id=1, replica_groups=mesh['hp'=2,'cp'=4] {'cp','hp'}, dimensions={0} | all-to-all | bytes 1048576 | tf_op jit(solution)/shard_map/all_to_all | solution.py:111
  215.9 36.5 %attend.6 = bf16[8,1,6,256,128]{4,3,2,1,0:T(8,128)(2,1)} custom-call(bf16[8,1,10,256,128]{4,3,2,1,0:T(8,128)(2,1)} %all-to-all-done.q_ref.do_ref.kv_ref, bf16[8,1,10,256,128]{4,3,2,1,0:T(8,128)(2,1)} %all-to-all-done.q_ref.do_ref.kv_ref, bf16[8,1,10,256,128]{4,3,2,1,0:T(8,128)(2,1)} %all-to-all-done.q_ref.do_ref.kv_ref, f32[8,8,2,1024]{3,2,1,0:T(2,128)} %all_to_all.55.st_ref), custom_call_target="tpu_custom_call" | custom-call | flops 12079595520 | bytes 10485760 | tf_op jit(solution)/shard_map/attend/pallas_call | solution.py:73
  252.5 78.9 %all-to-all-done.3.q_ref.do_ref.kv_ref = bf16[8,2,10,256,128]{4,3,2,1,0:T(8,128)(2,1)} async-done(((bf16[8,2,10,256,128]{4,3,2,1,0:T(8,128)(2,1)}), bf16[8,2,10,256,128]{4,3,2,1,0:T(8,128)(2,1)}, u32[]{:S(2)}, u32[]{:S(2)}) %all-to-all-start.3) | async-done | bytes 10485792 | tf_op jit(solution)/shard_map/all_to_all | solution.py:111
  334.2 4.0 copy.135
  341.4 9.3 %pad_maximum_fusion.2 = bf16[8,2,10,256,128]{4,3,2,1,0:T(8,128)(2,1)} fusion(bf16[8,2,1,256,128]{4,3,2,1,0:T(8,128)(2,1)S(1)} %get-tuple-element.135, bf16[8,2,1,256,128]{4,3,2,1,0:T(8,128)(2,1)S(1)} %get-tuple-element.136, bf16[8,2,4,256,128]{4,3,2,1,0:T(8,128)(2,1)S(1)} %get-tuple-element.133, bf16[8,2,4,256,128]{4,3,2,1,0:T(8,128)(2,1)S(1)} %get-tuple-element.134), kind=kLoop, calls=%fused_computation.3 | loop fusion | flops 15728640 | bytes 20971520 | tf_op jit(solution)/shard_map/concatenate | solution.py:120
  350.7 20.1 %all-to-all-done.4 = bf16[8,1,6,256,128]{4,3,2,1,0:T(8,128)(2,1)S(1)} async-done(((bf16[8,1,6,256,128]{4,3,2,1,0:T(8,128)(2,1)}), bf16[8,1,6,256,128]{4,3,2,1,0:T(8,128)(2,1)S(1)}, u32[]{:S(2)}, u32[]{:S(2)}) %all-to-all-start.4) | async-done | bytes 3145760 | tf_op jit(solution)/shard_map/all_to_all | solution.py:111
  370.8 4.1 all-to-all-start.5
  374.9 71.0 %attend.5 = bf16[8,2,6,256,128]{4,3,2,1,0:T(8,128)(2,1)} custom-call(bf16[8,2,10,256,128]{4,3,2,1,0:T(8,128)(2,1)} %all-to-all-done.1.q_ref.do_ref.kv_ref, bf16[8,2,10,256,128]{4,3,2,1,0:T(8,128)(2,1)} %all-to-all-done.1.q_ref.do_ref.kv_ref, bf16[8,2,10,256,128]{4,3,2,1,0:T(8,128)(2,1)} %all-to-all-done.1.q_ref.do_ref.kv_ref, ...), custom_call_target="tpu_custom_call" | custom-call | flops 24159191040 | bytes 20971520 | tf_op jit(solution)/shard_map/attend/pallas_call | solution.py:73
  454.9 6.2 pad.9
  461.1 29.2 %all-to-all-done.5.q_ref.do_ref.kv_ref = bf16[8,2,10,256,128]{4,3,2,1,0:T(8,128)(2,1)} async-done(((bf16[8,2,10,256,128]{4,3,2,1,0:T(8,128)(2,1)}), bf16[8,2,10,256,128]{4,3,2,1,0:T(8,128)(2,1)}, u32[]{:S(2)}, u32[]{:S(2)}) %all-to-all-start.5) | async-done | bytes 10485792 | tf_op jit(solution)/shard_map/all_to_all | solution.py:111
  493.8 71.0 %attend.8 = bf16[8,2,6,256,128]{4,3,2,1,0:T(8,128)(2,1)} custom-call(bf16[8,2,10,256,128]{4,3,2,1,0:T(8,128)(2,1)} %all-to-all-done.3.q_ref.do_ref.kv_ref, bf16[8,2,10,256,128]{4,3,2,1,0:T(8,128)(2,1)} %all-to-all-done.3.q_ref.do_ref.kv_ref, bf16[8,2,10,256,128]{4,3,2,1,0:T(8,128)(2,1)} %all-to-all-done.3.q_ref.do_ref.kv_ref, ...), custom_call_target="tpu_custom_call" | custom-call | flops 24159191040 | bytes 20971520 | tf_op jit(solution)/shard_map/attend/pallas_call | solution.py:73
  564.8 4.0 all-to-all-start.7
  574.6 7.7 copy.114
  592.2 47.1 %all-to-all-done.7 = bf16[8,2,6,256,128]{4,3,2,1,0:T(8,128)(2,1)} async-done(((bf16[8,2,6,256,128]{4,3,2,1,0:T(8,128)(2,1)}), bf16[8,2,6,256,128]{4,3,2,1,0:T(8,128)(2,1)}, u32[]{:S(2)}, u32[]{:S(2)}) %all-to-all-start.7) | async-done | bytes 6291488 | tf_op jit(solution)/shard_map/all_to_all | solution.py:111
  642.8 71.0 %attend.7 = bf16[8,2,6,256,128]{4,3,2,1,0:T(8,128)(2,1)} custom-call(bf16[8,2,10,256,128]{4,3,2,1,0:T(8,128)(2,1)} %all-to-all-done.5.q_ref.do_ref.kv_ref, bf16[8,2,10,256,128]{4,3,2,1,0:T(8,128)(2,1)} %all-to-all-done.5.q_ref.do_ref.kv_ref, bf16[8,2,10,256,128]{4,3,2,1,0:T(8,128)(2,1)} %all-to-all-done.5.q_ref.do_ref.kv_ref, ...), custom_call_target="tpu_custom_call" | custom-call | flops 24159191040 | bytes 20971520 | tf_op jit(solution)/shard_map/attend/pallas_call | solution.py:73
  717.4 7.7 copy.117
  734.9 36.5 %attend.9 = bf16[8,1,6,256,128]{4,3,2,1,0:T(8,128)(2,1)} custom-call(bf16[8,1,10,256,128]{4,3,2,1,0:T(8,128)(2,1)} %all-to-all-done.8.q_ref.do_ref.kv_ref, bf16[8,1,10,256,128]{4,3,2,1,0:T(8,128)(2,1)} %all-to-all-done.8.q_ref.do_ref.kv_ref, bf16[8,1,10,256,128]{4,3,2,1,0:T(8,128)(2,1)} %all-to-all-done.8.q_ref.do_ref.kv_ref, ...), custom_call_target="tpu_custom_call" | custom-call | flops 12079595520 | bytes 10485760 | tf_op jit(solution)/shard_map/attend/pallas_call | solution.py:73
  771.5 16.3 %all-to-all-done.9 = bf16[8,2,6,256,128]{4,3,2,1,0:T(8,128)(2,1)} async-done(((bf16[8,2,6,256,128]{4,3,2,1,0:T(8,128)(2,1)}), bf16[8,2,6,256,128]{4,3,2,1,0:T(8,128)(2,1)}, u32[]{:S(2)}, u32[]{:S(2)}) %all-to-all-start.9) | async-done | bytes 6291488 | tf_op jit(solution)/shard_map/all_to_all | solution.py:111
  790.4 7.7 copy.121
  807.9 18.8 %all-to-all-done.10 = bf16[8,1,6,256,128]{4,3,2,1,0:T(8,128)(2,1)S(1)} async-done(((bf16[8,1,6,256,128]{4,3,2,1,0:T(8,128)(2,1)}), bf16[8,1,6,256,128]{4,3,2,1,0:T(8,128)(2,1)S(1)}, u32[]{:S(2)}, u32[]{:S(2)}) %all-to-all-start.10) | async-done | bytes 3145760 | tf_op jit(solution)/shard_map/all_to_all | solution.py:111
  (95 shorter events, 99.4 us)
Async XLA Ops:
  18.2 63.7 %all-to-all-start = ((bf16[8,1,10,256,128]{4,3,2,1,0:T(8,128)(2,1)}), bf16[8,1,10,256,128]{4,3,2,1,0:T(8,128)(2,1)}, u32[]{:S(2)}, u32[]{:S(2)}) async-start(bf16[8,1,10,256,128]{4,3,2,1,0:T(8,128)(2,1)} %pad_maximum_fusion.3), calls=%async_computation | async-start | bytes 10485760 | tf_op jit(solution)/shard_map/all_to_all | solution.py:111
  22.8 10.1 %slice-start = ((s8[16777216]{0:T(1024)(128)(4,1)}), s8[4194304]{0:T(1024)(128)(4,1)S(1)}, s32[]{:S(2)}) async-start(s8[16777216]{0:T(1024)(128)(4,1)} %bitcast.148), calls=%async_computation.11 | async-start | bytes 8388608
  22.8 10.1 %slice-start.1 = ((s8[16777216]{0:T(1024)(128)(4,1)}), s8[4194304]{0:T(1024)(128)(4,1)S(1)}, s32[]{:S(2)}) async-start(s8[16777216]{0:T(1024)(128)(4,1)} %bitcast.148), calls=%async_computation.12 | async-start | bytes 8388608
  22.8 11.2 %slice-start.2 = ((s8[16777216]{0:T(1024)(128)(4,1)}), s8[4194304]{0:T(1024)(128)(4,1)S(1)}, s32[]{:S(2)}) async-start(s8[16777216]{0:T(1024)(128)(4,1)} %bitcast.148), calls=%async_computation.13 | async-start | bytes 8388608
  31.2 4.1 slice-start.3
  39.7 2.2 copy-start.4
  41.9 2.6 copy-start.5
  56.5 29.6 %copy-start.11 = (f32[8,32,256]{2,1,0:T(8,128)S(1)}, f32[8,32,256]{2,1,0:T(8,128)}, u32[]{:S(2)}) copy-start(f32[8,32,256]{2,1,0:T(8,128)} %param.11) | copy-start | bytes 786436
  82.0 119.5 %all-to-all-start.1 = ((bf16[8,2,10,256,128]{4,3,2,1,0:T(8,128)(2,1)}), bf16[8,2,10,256,128]{4,3,2,1,0:T(8,128)(2,1)}, u32[]{:S(2)}, u32[]{:S(2)}) async-start(bf16[8,2,10,256,128]{4,3,2,1,0:T(8,128)(2,1)} %pad_maximum_fusion.1), calls=%async_computation.1 | async-start | bytes 20971520 | tf_op jit(solution)/shard_map/all_to_all | solution.py:111
  103.4 4.0 copy-start.1
  107.4 1.6 copy-start.10
  212.0 119.3 %all-to-all-start.3 = ((bf16[8,2,10,256,128]{4,3,2,1,0:T(8,128)(2,1)}), bf16[8,2,10,256,128]{4,3,2,1,0:T(8,128)(2,1)}, u32[]{:S(2)}, u32[]{:S(2)}) async-start(bf16[8,2,10,256,128]{4,3,2,1,0:T(8,128)(2,1)} %pad_maximum_fusion), calls=%async_computation.3 | async-start | bytes 20971520 | tf_op jit(solution)/shard_map/all_to_all | solution.py:111
  331.4 39.4 %all-to-all-start.4 = ((bf16[8,1,6,256,128]{4,3,2,1,0:T(8,128)(2,1)}), bf16[8,1,6,256,128]{4,3,2,1,0:T(8,128)(2,1)S(1)}, u32[]{:S(2)}, u32[]{:S(2)}) async-start(bf16[8,1,6,256,128]{4,3,2,1,0:T(8,128)(2,1)} %attend.6), calls=%async_computation.4 | async-start | bytes 6291456 | tf_op jit(solution)/shard_map/all_to_all | solution.py:111
  334.2 4.0 copy-start
  338.1 1.7 copy-start.6
  338.2 1.7 copy-start.7
  370.8 119.5 %all-to-all-start.5 = ((bf16[8,2,10,256,128]{4,3,2,1,0:T(8,128)(2,1)}), bf16[8,2,10,256,128]{4,3,2,1,0:T(8,128)(2,1)}, u32[]{:S(2)}, u32[]{:S(2)}) async-start(bf16[8,2,10,256,128]{4,3,2,1,0:T(8,128)(2,1)} %pad_maximum_fusion.2), calls=%async_computation.5 | async-start | bytes 20971520 | tf_op jit(solution)/shard_map/all_to_all | solution.py:111
  490.3 74.5 %all-to-all-start.6 = ((bf16[8,2,6,256,128]{4,3,2,1,0:T(8,128)(2,1)}), bf16[8,2,6,256,128]{4,3,2,1,0:T(8,128)(2,1)}, u32[]{:S(2)}, u32[]{:S(2)}) async-start(bf16[8,2,6,256,128]{4,3,2,1,0:T(8,128)(2,1)} %attend.5), calls=%async_computation.6 | async-start | bytes 12582912 | tf_op jit(solution)/shard_map/all_to_all | solution.py:111
  564.8 4.1 copy-start.2
  564.8 74.4 %all-to-all-start.7 = ((bf16[8,2,6,256,128]{4,3,2,1,0:T(8,128)(2,1)}), bf16[8,2,6,256,128]{4,3,2,1,0:T(8,128)(2,1)}, u32[]{:S(2)}, u32[]{:S(2)}) async-start(bf16[8,2,6,256,128]{4,3,2,1,0:T(8,128)(2,1)} %attend.8), calls=%async_computation.7 | async-start | bytes 12582912 | tf_op jit(solution)/shard_map/all_to_all | solution.py:111
  568.9 1.6 copy-start.3
  568.9 2.4 copy-start.8
  568.9 2.4 copy-start.9
  639.2 74.6 %all-to-all-start.8 = ((bf16[8,1,10,256,128]{4,3,2,1,0:T(8,128)(2,1)}), bf16[8,1,10,256,128]{4,3,2,1,0:T(8,128)(2,1)}, u32[]{:S(2)}, u32[]{:S(2)}) async-start(bf16[8,1,10,256,128]{4,3,2,1,0:T(8,128)(2,1)} %pad_maximum_fusion.4), calls=%async_computation.8 | async-start | bytes 10485760 | tf_op jit(solution)/shard_map/all_to_all | solution.py:111
  713.8 73.9 %all-to-all-start.9 = ((bf16[8,2,6,256,128]{4,3,2,1,0:T(8,128)(2,1)}), bf16[8,2,6,256,128]{4,3,2,1,0:T(8,128)(2,1)}, u32[]{:S(2)}, u32[]{:S(2)}) async-start(bf16[8,2,6,256,128]{4,3,2,1,0:T(8,128)(2,1)} %attend.7), calls=%async_computation.9 | async-start | bytes 12582912 | tf_op jit(solution)/shard_map/all_to_all | solution.py:111
  787.7 39.0 %all-to-all-start.10 = ((bf16[8,1,6,256,128]{4,3,2,1,0:T(8,128)(2,1)}), bf16[8,1,6,256,128]{4,3,2,1,0:T(8,128)(2,1)S(1)}, u32[]{:S(2)}, u32[]{:S(2)}) async-start(bf16[8,1,6,256,128]{4,3,2,1,0:T(8,128)(2,1)} %attend.9), calls=%async_computation.10 | async-start | bytes 6291456 | tf_op jit(solution)/shard_map/all_to_all | solution.py:111

commit v2 on v1

--- a/solution.py
+++ b/solution.py
@@ -9,10 +9,10 @@
 from jax.sharding import PartitionSpec as P
 
 AXES = ('cp', 'hp')
-CHUNKS = (1, 2, 2, 2, 1)
+CHUNKS = (1, 3, 3, 1)
 ORDER = (
     ('in', 0, ()), ('in', 1, ()), ('stat', 0, ()), ('in', 2, ()), ('out', 0, ()), ('in', 3, (0,)), ('out', 1, ()),
-    ('out', 2, (1,)), ('in', 4, ()), ('out', 3, (2,)), ('out', 4, (3,)),
+    ('out', 2, (1,)), ('out', 3, (2,)),
 )
 
 
@@ -134,12 +134,17 @@
                 return [lax.pad(x, zero, [(lo, b - hi, 0)] + [(0, 0, 0)] * 3) for x in new]
             return [lax.dynamic_update_slice(out, x, (lo, 0, 0, 0)) for out, x in zip(outs, new)]
 
-        got, back, ahead, st, outs, last, prev = {}, {}, {}, None, None, None, None
+        def attend(c):
+            return _attend(got[c], st, bounds[c][0], g, scale)
+
+        got, back, ahead, ahead_out, st, outs, last, prev = {}, {}, {}, {}, None, None, None, None
         for kind, c, done in ORDER:
             if kind == 'in':
                 x = ahead[c] if c in ahead else pack(c)
             elif kind == 'out':
-                x = _attend(got[c], st, bounds[c][0], g, scale)
+                x = ahead_out[c] if c in ahead_out else attend(c)
+                if c == 0:
+                    x, ahead_out[1] = lax.optimization_barrier((x, attend(1)))
             else:
                 dlt = jnp.sum(do.astype(jnp.float32) * o.astype(jnp.float32), axis=-1).transpose(0, 2, 1)
                 x = jnp.stack([z.reshape(b, hk, g * t).transpose(1, 0, 2) for z in (lse, dlt)], axis=2)

time: 837 us -> 818 us (0.977)
  local copies, waits for them, and re-layouts: 131 us -> 168 us
  waiting for transfers between devices: 317 us -> 283 us
  other arithmetic: 49.8 us -> 36.2 us
    all_to_all x10 -> x8, waiting for transfers between devices: 317 us -> 283 us  [exchange(): return lax.all_to_all(x, AXES, 0, 0, tiled=True)]
    concatenate x5 -> x4, other arithmetic: 34 us -> 20.3 us  [pack(): jnp.concatenate([heads(x, *bounds[c]) for x in (q, do, k, v)], axis=2)]
    transpose x10 -> x8, local copies, waits for them, and re-layouts: 20.8 us -> 33.4 us  [unpack(): y[:, :, :g].transpose(1, 3, 0, 2, 4).reshape(hi - lo, t, hq, d)]
    optimization_barrier x4 -> x3, local copies, waits for them, and re-layouts: 25.1 us -> 33 us  [body(): back[e], x = lax.optimization_barrier((back[e], x))]
    unnamed x38 -> x40, local copies, waits for them, and re-layouts: 19.6 us -> 26.2 us
    all_to_all x10 -> x8, starting transfers between devices: 36.6 us -> 31 us  [exchange(): return lax.all_to_all(x, AXES, 0, 0, tiled=True)]
    pallas_call x5 -> x4, Pallas kernels: 286 us -> 284 us  [_attend(): pl.pallas_call(functools.partial(_kernel, n, g, scale), grid=(nb, n), in_...]
    dynamic_update_slice x9 -> x7, local copies, waits for them, and re-layouts: 16.5 us -> 19 us  [unpack(): lax.dynamic_update_slice(out, x, (lo, 0, 0, 0))]
  transfers between devices with their start and end apart: 10 -> 8, of which waited for: 8 -> 6; matrix products, arithmetic and copies ran while one was open for 18% -> 22% of each run, Pallas kernels for 34% -> 35%
where the time goes in v2:
time: 818 us; the launch traced here: 814 us
  Pallas kernels  284 us (35%)
  waiting for transfers between devices  283 us (35%)
  local copies, waits for them, and re-layouts  168 us (21%)
  other arithmetic  36.2 us (4%)
  starting transfers between devices  31 us (4%)
  blocking collectives  10.5 us (1%)
    pallas_call x4, Pallas kernels, _attend(): pl.pallas_call(functools.partial(_kernel, n, g, scale), grid=(nb, n), in_...  284 us
    all_to_all x8, waiting for transfers between devices, exchange(): return lax.all_to_all(x, AXES, 0, 0, tiled=True)  283 us
    slice x12, local copies, waits for them, and re-layouts, heads(): x = x[lo:hi]  37.8 us
    transpose x8, local copies, waits for them, and re-layouts, unpack(): y[:, :, :g].transpose(1, 3, 0, 2, 4).reshape(hi - lo, t, hq, d)  33.4 us
    optimization_barrier x3, local copies, waits for them, and re-layouts, body(): back[e], x = lax.optimization_barrier((back[e], x))  33 us
    all_to_all x8, starting transfers between devices, exchange(): return lax.all_to_all(x, AXES, 0, 0, tiled=True)  31 us
    unnamed x40, local copies, waits for them, and re-layouts  26.2 us
    concatenate x4, other arithmetic, pack(): jnp.concatenate([heads(x, *bounds[c]) for x in (q, do, k, v)], axis=2)  20.3 us
  transfers between devices with their start and end apart: 8, of which 6 were waited for; matrix products, arithmetic and copies ran while one was open for 22% of the time, Pallas kernels for 35%

profile of v2, /device:TPU:0, one launch (start us, length us, event | category | flops | bytes accessed | tf_op | source)
XLA Modules:
  0.0 813.9 jit_solution(16961024465871672895)
XLA Ops:
  4.8 4.3 fusion.6
  9.9 4.3 fusion.7
  18.3 4.9 all-to-all-start
  23.2 11.9 %fusion.8 = (bf16[3,256,32,128]{3,2,1,0:T(8,128)(2,1)}, bf16[3,256,32,128]{3,2,1,0:T(8,128)(2,1)}) fusion(bf16[8,256,32,128]{3,2,1,0:T(8,128)(2,1)} %param.6), kind=kLoop, calls=%fused_computation.43 | loop fusion | bytes 25165824 | tf_op jit(solution)/shard_map/slice | solution.py:107
  35.1 8.0 copy.102
  43.2 5.5 fusion.9
  48.7 5.4 copy.103
  59.5 7.0 pad_maximum_fusion
  66.5 15.9 %all-to-all-done.q_ref.do_ref.kv_ref = bf16[8,1,10,256,128]{4,3,2,1,0:T(8,128)(2,1)} async-done(((bf16[8,1,10,256,128]{4,3,2,1,0:T(8,128)(2,1)}), bf16[8,1,10,256,128]{4,3,2,1,0:T(8,128)(2,1)}, u32[]{:S(2)}, u32[]{:S(2)}) %all-to-all-start) | async-done | bytes 5242912 | tf_op jit(solution)/shard_map/all_to_all | solution.py:111
  82.4 4.5 all-to-all-start.1
  88.1 15.4 %multiply_reduce_fusion = f32[8,256,32]{2,1,0:T(8,128)S(1)} fusion(bf16[8,256,32,128]{3,2,1,0:T(8,128)(2,1)} %param.9, bf16[8,256,32,128]{3,2,1,0:T(8,128)(2,1)} %param.10), kind=kLoop, calls=%fused_computation | loop fusion | flops 33488896 | bytes 33816576 | tf_op jit(solution)/shard_map/reduce_sum | solution.py:149
  104.2 5.4 copy.108
  109.6 5.1 copy.109
  118.7 7.1 pad_maximum_fusion.1
  125.8 132.8 %all-to-all-done.1.q_ref.do_ref.kv_ref = bf16[8,3,10,256,128]{4,3,2,1,0:T(8,128)(2,1)} async-done(((bf16[8,3,10,256,128]{4,3,2,1,0:T(8,128)(2,1)}), bf16[8,3,10,256,128]{4,3,2,1,0:T(8,128)(2,1)}, u32[]{:S(2)}, u32[]{:S(2)}) %all-to-all-start.1) | async-done | bytes 15728672 | tf_op jit(solution)/shard_map/all_to_all | solution.py:111
  258.6 10.5 %all_to_all.45.st_ref = f32[8,8,2,1024]{3,2,1,0:T(2,128)} all-to-all(f32[8,8,2,1024]{3,2,1,0:T(2,128)S(1)} %pad_maximum_fusion.4), channel_id=1, replica_groups=mesh['hp'=2,'cp'=4] {'cp','hp'}, dimensions={0} | all-to-all | bytes 1048576 | tf_op jit(solution)/shard_map/all_to_all | solution.py:111
  269.1 4.6 all-to-all-start.3
  273.8 36.5 %attend.4 = bf16[8,1,6,256,128]{4,3,2,1,0:T(8,128)(2,1)} custom-call(bf16[8,1,10,256,128]{4,3,2,1,0:T(8,128)(2,1)} %all-to-all-done.q_ref.do_ref.kv_ref, bf16[8,1,10,256,128]{4,3,2,1,0:T(8,128)(2,1)} %all-to-all-done.q_ref.do_ref.kv_ref, bf16[8,1,10,256,128]{4,3,2,1,0:T(8,128)(2,1)} %all-to-all-done.q_ref.do_ref.kv_ref, f32[8,8,2,1024]{3,2,1,0:T(2,128)} %all_to_all.45.st_ref), custom_call_target="tpu_custom_call" | custom-call | flops 12079595520 | bytes 10485760 | tf_op jit(solution)/shard_map/attend/pallas_call | solution.py:73
  310.3 105.2 %attend.5 = bf16[8,3,6,256,128]{4,3,2,1,0:T(8,128)(2,1)} custom-call(bf16[8,3,10,256,128]{4,3,2,1,0:T(8,128)(2,1)} %all-to-all-done.1.q_ref.do_ref.kv_ref, bf16[8,3,10,256,128]{4,3,2,1,0:T(8,128)(2,1)} %all-to-all-done.1.q_ref.do_ref.kv_ref, bf16[8,3,10,256,128]{4,3,2,1,0:T(8,128)(2,1)} %all-to-all-done.1.q_ref.do_ref.kv_ref, ...), custom_call_target="tpu_custom_call" | custom-call | flops 36238786560 | bytes 31457280 | tf_op jit(solution)/shard_map/attend/pallas_call | solution.py:73
  415.5 30.0 %all-to-all-done.3.q_ref.do_ref.kv_ref = bf16[8,3,10,256,128]{4,3,2,1,0:T(8,128)(2,1)} async-done(((bf16[8,3,10,256,128]{4,3,2,1,0:T(8,128)(2,1)}), bf16[8,3,10,256,128]{4,3,2,1,0:T(8,128)(2,1)}, u32[]{:S(2)}, u32[]{:S(2)}) %all-to-all-start.3) | async-done | bytes 15728672 | tf_op jit(solution)/shard_map/all_to_all | solution.py:111
  454.6 29.9 %all-to-all-done.4 = bf16[8,1,6,256,128]{4,3,2,1,0:T(8,128)(2,1)S(1)} async-done(((bf16[8,1,6,256,128]{4,3,2,1,0:T(8,128)(2,1)}), bf16[8,1,6,256,128]{4,3,2,1,0:T(8,128)(2,1)S(1)}, u32[]{:S(2)}, u32[]{:S(2)}) %all-to-all-start.4) | async-done | bytes 3145760 | tf_op jit(solution)/shard_map/all_to_all | solution.py:111
  497.4 6.2 pad.9
  503.6 43.9 %all-to-all-done.5.q_ref.do_ref.kv_ref = bf16[8,1,10,256,128]{4,3,2,1,0:T(8,128)(2,1)} async-done(((bf16[8,1,10,256,128]{4,3,2,1,0:T(8,128)(2,1)}), bf16[8,1,10,256,128]{4,3,2,1,0:T(8,128)(2,1)}, u32[]{:S(2)}, u32[]{:S(2)}) %all-to-all-start.5) | async-done | bytes 5242912 | tf_op jit(solution)/shard_map/all_to_all | solution.py:111
  551.3 105.2 %attend.7 = bf16[8,3,6,256,128]{4,3,2,1,0:T(8,128)(2,1)} custom-call(bf16[8,3,10,256,128]{4,3,2,1,0:T(8,128)(2,1)} %all-to-all-done.3.q_ref.do_ref.kv_ref, bf16[8,3,10,256,128]{4,3,2,1,0:T(8,128)(2,1)} %all-to-all-done.3.q_ref.do_ref.kv_ref, bf16[8,3,10,256,128]{4,3,2,1,0:T(8,128)(2,1)} %all-to-all-done.3.q_ref.do_ref.kv_ref, ...), custom_call_target="tpu_custom_call" | custom-call | flops 36238786560 | bytes 31457280 | tf_op jit(solution)/shard_map/attend/pallas_call | solution.py:73
  660.3 36.6 %attend.6 = bf16[8,1,6,256,128]{4,3,2,1,0:T(8,128)(2,1)} custom-call(bf16[8,1,10,256,128]{4,3,2,1,0:T(8,128)(2,1)} %all-to-all-done.5.q_ref.do_ref.kv_ref, bf16[8,1,10,256,128]{4,3,2,1,0:T(8,128)(2,1)} %all-to-all-done.5.q_ref.do_ref.kv_ref, bf16[8,1,10,256,128]{4,3,2,1,0:T(8,128)(2,1)} %all-to-all-done.5.q_ref.do_ref.kv_ref, ...), custom_call_target="tpu_custom_call" | custom-call | flops 12079595520 | bytes 10485760 | tf_op jit(solution)/shard_map/attend/pallas_call | solution.py:73
  697.0 15.4 %copy.94 = bf16[8,3,6,256,128]{4,0,3,1,2:T(8,128)(2,1)} copy(bf16[8,3,6,256,128]{4,3,2,1,0:T(8,128)(2,1)} %all-to-all-done.6) | data formatting | bytes 18874368 | tf_op jit(solution)/shard_map/optimization_barrier | solution.py:161
  712.4 6.2 slice_bitcast_fusion.1
  718.6 7.8 copy.93
  734.0 30.5 %all-to-all-done.7 = bf16[8,3,6,256,128]{4,3,2,1,0:T(8,128)(2,1)} async-done(((bf16[8,3,6,256,128]{4,3,2,1,0:T(8,128)(2,1)}), bf16[8,3,6,256,128]{4,3,2,1,0:T(8,128)(2,1)}, u32[]{:S(2)}, u32[]{:S(2)}) %all-to-all-start.7) | async-done | bytes 9437216 | tf_op jit(solution)/shard_map/all_to_all | solution.py:111
  767.7 15.5 %copy.98 = bf16[8,3,6,256,128]{4,0,3,1,2:T(8,128)(2,1)} copy(bf16[8,3,6,256,128]{4,3,2,1,0:T(8,128)(2,1)} %all-to-all-done.7) | data formatting | bytes 18874368 | tf_op jit(solution)/shard_map/optimization_barrier | solution.py:161
  783.2 6.3 slice_bitcast_fusion
  789.5 7.9 copy.96
  (86 shorter events, 76.7 us)
Async XLA Ops:
  18.3 64.1 %all-to-all-start = ((bf16[8,1,10,256,128]{4,3,2,1,0:T(8,128)(2,1)}), bf16[8,1,10,256,128]{4,3,2,1,0:T(8,128)(2,1)}, u32[]{:S(2)}, u32[]{:S(2)}) async-start(bf16[8,1,10,256,128]{4,3,2,1,0:T(8,128)(2,1)} %pad_maximum_fusion.2), calls=%async_computation | async-start | bytes 10485760 | tf_op jit(solution)/shard_map/all_to_all | solution.py:111
  23.2 20.0 %slice-start = ((s8[16777216]{0:T(1024)(128)(4,1)}), s8[4194304]{0:T(1024)(128)(4,1)S(1)}, s32[]{:S(2)}) async-start(s8[16777216]{0:T(1024)(128)(4,1)} %bitcast.119), calls=%async_computation.9 | async-start | bytes 8388608
  23.2 20.0 %slice-start.1 = ((s8[16777216]{0:T(1024)(128)(4,1)}), s8[4194304]{0:T(1024)(128)(4,1)S(1)}, s32[]{:S(2)}) async-start(s8[16777216]{0:T(1024)(128)(4,1)} %bitcast.119), calls=%async_computation.10 | async-start | bytes 8388608
  23.2 20.0 %slice-start.2 = ((s8[16777216]{0:T(1024)(128)(4,1)}), s8[4194304]{0:T(1024)(128)(4,1)S(1)}, s32[]{:S(2)}) async-start(s8[16777216]{0:T(1024)(128)(4,1)} %bitcast.119), calls=%async_computation.11 | async-start | bytes 8388608
  35.1 8.1 slice-start.3
  48.7 5.4 copy-start.4
  48.7 6.8 copy-start.5
  54.0 3.5 slice-start.6
  55.5 2.8 slice-start.7
  66.5 20.5 %copy-start.9 = (f32[8,32,256]{2,1,0:T(8,128)S(1)}, f32[8,32,256]{2,1,0:T(8,128)}, u32[]{:S(2)}) copy-start(f32[8,32,256]{2,1,0:T(8,128)} %param.11) | copy-start | bytes 786436
  82.4 176.3 %all-to-all-start.1 = ((bf16[8,3,10,256,128]{4,3,2,1,0:T(8,128)(2,1)}), bf16[8,3,10,256,128]{4,3,2,1,0:T(8,128)(2,1)}, u32[]{:S(2)}, u32[]{:S(2)}) async-start(bf16[8,3,10,256,128]{4,3,2,1,0:T(8,128)(2,1)} %pad_maximum_fusion), calls=%async_computation.1 | async-start | bytes 31457280 | tf_op jit(solution)/shard_map/all_to_all | solution.py:111
  103.4 6.1 slice-start.4
  104.2 5.4 slice-start.5
  109.6 5.1 copy-start.8
  109.6 5.6 copy-start.2
  109.6 5.6 copy-start.3
  114.7 2.8 copy-start
  269.1 176.3 %all-to-all-start.3 = ((bf16[8,3,10,256,128]{4,3,2,1,0:T(8,128)(2,1)}), bf16[8,3,10,256,128]{4,3,2,1,0:T(8,128)(2,1)}, u32[]{:S(2)}, u32[]{:S(2)}) async-start(bf16[8,3,10,256,128]{4,3,2,1,0:T(8,128)(2,1)} %pad_maximum_fusion.1), calls=%async_computation.3 | async-start | bytes 31457280 | tf_op jit(solution)/shard_map/all_to_all | solution.py:111
  445.5 39.0 %all-to-all-start.4 = ((bf16[8,1,6,256,128]{4,3,2,1,0:T(8,128)(2,1)}), bf16[8,1,6,256,128]{4,3,2,1,0:T(8,128)(2,1)S(1)}, u32[]{:S(2)}, u32[]{:S(2)}) async-start(bf16[8,1,6,256,128]{4,3,2,1,0:T(8,128)(2,1)} %attend.4), calls=%async_computation.4 | async-start | bytes 6291456 | tf_op jit(solution)/shard_map/all_to_all | solution.py:111
  447.9 2.6 copy-start.1
  447.9 3.4 copy-start.6
  447.9 3.4 copy-start.7
  484.5 63.0 %all-to-all-start.5 = ((bf16[8,1,10,256,128]{4,3,2,1,0:T(8,128)(2,1)}), bf16[8,1,10,256,128]{4,3,2,1,0:T(8,128)(2,1)}, u32[]{:S(2)}, u32[]{:S(2)}) async-start(bf16[8,1,10,256,128]{4,3,2,1,0:T(8,128)(2,1)} %pad_maximum_fusion.3), calls=%async_computation.5 | async-start | bytes 10485760 | tf_op jit(solution)/shard_map/all_to_all | solution.py:111
  547.5 109.0 %all-to-all-start.6 = ((bf16[8,3,6,256,128]{4,3,2,1,0:T(8,128)(2,1)}), bf16[8,3,6,256,128]{4,3,2,1,0:T(8,128)(2,1)}, u32[]{:S(2)}, u32[]{:S(2)}) async-start(bf16[8,3,6,256,128]{4,3,2,1,0:T(8,128)(2,1)} %attend.5), calls=%async_computation.6 | async-start | bytes 18874368 | tf_op jit(solution)/shard_map/all_to_all | solution.py:111
  656.5 108.0 %all-to-all-start.7 = ((bf16[8,3,6,256,128]{4,3,2,1,0:T(8,128)(2,1)}), bf16[8,3,6,256,128]{4,3,2,1,0:T(8,128)(2,1)}, u32[]{:S(2)}, u32[]{:S(2)}) async-start(bf16[8,3,6,256,128]{4,3,2,1,0:T(8,128)(2,1)} %attend.7), calls=%async_computation.7 | async-start | bytes 18874368 | tf_op jit(solution)/shard_map/all_to_all | solution.py:111
  764.5 40.4 %all-to-all-start.8 = ((bf16[8,1,6,256,128]{4,3,2,1,0:T(8,128)(2,1)}), bf16[8,1,6,256,128]{4,3,2,1,0:T(8,128)(2,1)}, u32[]{:S(2)}, u32[]{:S(2)}) async-start(bf16[8,1,6,256,128]{4,3,2,1,0:T(8,128)(2,1)} %attend.6), calls=%async_computation.8 | async-start | bytes 6291456 | tf_op jit(solution)/shard_map/all_to_all | solution.py:111
